TPU v7x, 32 devices: a whole 2x2x4 slice. The times are simulated.
32 devices in a mesh: rows: 8 (over y, x, core), cols: 4 (over z).
Axes of the slice: x: 2, y: 2, z: 4, core: 2. Of those that a mesh axis runs over, the one named last changes fastest.
Arguments:
- token_ids: int32 [16, 2048], P('rows', 'cols'), may hold values from 0 to 131071, as said below
- lengths: int32 [16], P('rows'), may hold values from 1 to 2048
- table: bfloat16 [131072, 512], P('rows', 'cols'), may hold values from -6 to 6
- attn_gain: float32 [512], replicated, may hold values from 0.1 to 1.9
- w_qkv: bfloat16 [512, 1536], replicated, may hold values from -2 to 2
- w_out: bfloat16 [512, 512], replicated, may hold values from -0.25 to 0.25
- mlp_gain: float32 [512], replicated, may hold values from 0.1 to 1.9
- w_in: bfloat16 [512, 4096], replicated, may hold values from -0.25 to 0.25
- w_down: bfloat16 [2048, 512], replicated, may hold values from -0.125 to 0.125
Outputs:
- layer_out: bfloat16 [16, 2048, 512], P('rows', 'cols')
Inputs may be any that keep to these rules, and one draw needn't show every extreme that they name: `token_ids`: ids lie in 0 to 131071. In each aligned block of 2 histories (4096 positions) at most 1365 ids fall in any one block of 16384 consecutive table rows, and in every such block of histories some block of table rows receives exactly 1365.
All inputs are finite; a program needn't handle non-finite values.
Results may differ from a plain program's by a relative error of at most 0.012.
Values may be sent and summed in bfloat16 or wider, within the bound.
A program may use at most 192 MiB of HBM per device.

v0:
```python
import jax
import jax.numpy as jnp
from jax import lax
from jax.sharding import PartitionSpec as P

D = 512
HEADS = 8
FF = 2048


def rms_norm(values_f32, gain):
    mean_sq = jnp.mean(values_f32 * values_f32, axis=-1, keepdims=True)
    return values_f32 * lax.rsqrt(mean_sq + 1e-06) * gain


def local(token_ids, lengths, table, attn_gain, w_qkv, w_out, mlp_gain, w_in, w_down):
    batch_dev, quarter = token_ids.shape
    col_count = lax.axis_size("cols")
    row_count = lax.axis_size("rows")
    full_len = quarter * col_count
    block_rows, col_width = table.shape
    zero_bf = jnp.zeros((), jnp.bfloat16)
    own_ids = lax.all_gather(token_ids, "cols", axis=1, tiled=True)
    flat_ids = own_ids.reshape(-1)
    token_count = flat_ids.shape[0]
    capacity = 8 * token_count // (3 * row_count)
    owner_block = flat_ids // block_rows
    onehot = (owner_block[:, None] == jnp.arange(row_count, dtype=jnp.int32)[None, :]).astype(
        jnp.int32
    )
    slot_rank = jnp.sum((jnp.cumsum(onehot, axis=0) - 1) * onehot, axis=1)
    slot_index = owner_block * capacity + slot_rank
    requests = jnp.full((row_count * capacity,), -1, jnp.int32)
    requests = (
        requests.at[slot_index]
        .set(flat_ids - owner_block * block_rows)
        .reshape(row_count, capacity)
    )
    asked = lax.all_to_all(requests, "rows", split_axis=0, concat_axis=0, tiled=True)
    looked = jnp.take(table, jnp.maximum(asked, 0), axis=0)
    looked = jnp.where((asked >= 0)[..., None], looked, zero_bf)
    returned = lax.all_to_all(looked, "rows", split_axis=0, concat_axis=0, tiled=True)
    embedded = returned.reshape(row_count * capacity, col_width)[slot_index]
    embedded = embedded.reshape(batch_dev, full_len, col_width)
    sequence = lax.all_to_all(embedded, "cols", split_axis=1, concat_axis=2, tiled=True)
    residual = sequence.astype(jnp.float32)
    normed = rms_norm(residual, attn_gain).astype(jnp.bfloat16)
    projected = jnp.einsum("bqe,ef->bqf", normed, w_qkv, preferred_element_type=jnp.float32).astype(
        jnp.bfloat16
    )
    head_dim = D // HEADS
    queries = projected[..., :D].reshape(batch_dev, quarter, HEADS, head_dim)
    keys = projected[..., D : 2 * D]
    values = projected[..., 2 * D :]
    query_pos = lax.axis_index("cols") * quarter + jnp.arange(quarter, dtype=jnp.int32)
    running_max = jnp.full((batch_dev, HEADS, quarter), -1e30, jnp.float32)
    key_piece = lax.all_gather(keys, "cols", axis=1, tiled=True)
    value_piece = lax.all_gather(values, "cols", axis=1, tiled=True)
    piece_len = key_piece.shape[1]
    key_heads = key_piece.reshape(batch_dev, piece_len, HEADS, head_dim)
    value_heads = value_piece.reshape(batch_dev, piece_len, HEADS, head_dim)
    scores = (
        jnp.einsum("bqhd,bkhd->bhqk", queries, key_heads, preferred_element_type=jnp.float32)
        * 0.125
    )
    key_pos = jnp.arange(piece_len, dtype=jnp.int32)
    causal = key_pos[None, :] <= query_pos[:, None]
    inside = key_pos[None, :] < lengths[:, None]
    valid = causal[None, None, :, :] & inside[:, None, None, :]
    scores = jnp.where(valid, scores, -1e30)
    new_max = jnp.maximum(running_max, jnp.max(scores, axis=-1))
    probs = jnp.where(valid, jnp.exp(scores - new_max[..., None]), 0.0)
    running_sum = jnp.sum(probs, axis=-1)
    weighted = jnp.einsum(
        "bhqk,bkhd->bhqd",
        probs.astype(jnp.bfloat16),
        value_heads,
        preferred_element_type=jnp.float32,
    )
    final_max, final_sum, weighted = (new_max, running_sum, weighted)
    summed = weighted / final_sum[..., None]
    attended = (
        jnp.transpose(summed, (0, 2, 1, 3)).reshape(batch_dev, quarter, D).astype(jnp.bfloat16)
    )
    hidden = (
        residual + jnp.einsum("bqe,ef->bqf", attended, w_out, preferred_element_type=jnp.float32)
    ).astype(jnp.bfloat16)
    hidden_f32 = hidden.astype(jnp.float32)
    normed_two = rms_norm(hidden_f32, mlp_gain).astype(jnp.bfloat16)
    gate_up = jnp.einsum("bqe,ef->bqf", normed_two, w_in, preferred_element_type=jnp.float32)
    act = (jax.nn.silu(gate_up[..., :FF]) * gate_up[..., FF:]).astype(jnp.bfloat16)
    return (
        hidden_f32 + jnp.einsum("bqf,fe->bqe", act, w_down, preferred_element_type=jnp.float32)
    ).astype(jnp.bfloat16)


def solution(mesh):
    in_specs = (P("rows", "cols"), P("rows"), P("rows", "cols"), P(), P(), P(), P(), P(), P())
    out_specs = P("rows", "cols", None)
    return jax.shard_map(local, mesh=mesh, in_specs=in_specs, out_specs=out_specs, check_vma=False)
```

profile of v0, /device:TPU:0, one launch (start us, length us, event | category | flops | bytes accessed | tf_op | source)
XLA Modules:
  0.0 414.5 jit_solution(13161058633130101524)
XLA Ops:
  6.5 0.0 copy-start
  6.5 15.2 %all_gather.9 = s32[2,2048]{1,0:T(2,128)S(1)} all-gather(s32[2,512]{1,0:T(2,128)} %param.9), channel_id=1, replica_groups=mesh['rows'=8,'cols'=4] {'cols'}, dimensions={1}, use_global_device_ids=true | all-gather | bytes 20480 | tf_op jit(solution)/shard_map/all_gather | solution.py:23
  21.8 2.3 reduce-window.6
  24.1 0.3 slice_reduce_fusion
  24.4 0.2 reduce-window.9
  24.6 0.1 add_bitcast_fusion
  24.8 0.1 fusion.32
  24.9 0.1 compare_select_fusion
  25.0 15.5 %scatter_custom_fusion = s32[10920]{0:T(1024)S(1)} fusion(s32[4096]{0:T(1024)S(1)} %bitcast.81, s32[4096]{0:T(1024)S(1)} %get-tuple-element.10, s32[]{:T(128)} %constant.27.clone.1), kind=kCustom, calls=%fused_computation.65 | custom fusion | bytes 43684 | tf_op jit(solution)/shard_map/scatter | solution.py:36
  40.5 0.1 all_to_all.16
  40.6 8.4 %all_to_all.23 = s32[8,1,1365]{2,1,0:T(1,128)S(1)} all-to-all(s32[8,1,1365]{2,1,0:T(1,128)S(1)} %all_to_all.16), channel_id=1, replica_groups=mesh['rows'=8,'cols'=4] {'rows'}, dimensions={0} | all-to-all | bytes 87360 | tf_op jit(solution)/shard_map/all_to_all | solution.py:39
  49.1 0.1 reshape.265
  49.2 23.7 %gather_fusion = bf16[10920,128]{1,0:T(8,128)(2,1)} fusion(bf16[16384,128]{1,0:T(8,128)(2,1)} %param.11, s32[11264]{0:T(1024)S(1)} %pad_clamp_fusion), kind=kCustom, calls=%fused_computation | custom fusion | bytes 5634720 | tf_op jit(solution)/shard_map/jit(_take)/gather | solution.py:40
  72.9 4.2 %reshape.264 = bf16[8,1365,128]{2,1,0:T(8,128)(2,1)} reshape(bf16[10920,128]{1,0:T(8,128)(2,1)} %gather_fusion) | data formatting | bytes 5591040 | tf_op jit(solution)/shard_map/jit(_take)/gather | solution.py:40
  77.1 10.2 %select_select_fusion = bf16[8,1365,128]{2,1,0:T(8,128)(2,1)} fusion(bf16[8,1365,128]{2,1,0:T(8,128)(2,1)} %reshape.264, pred[8,1365]{1,0:T(8,128)(4,1)S(1)} %get-tuple-element.9, pred[8,1365]{1,0:T(8,128)(4,1)S(1)} %get-tuple-element.8), kind=kLoop, calls=%fused_computation.21 | loop fusion | flops 2795520 | bytes 5612880 | tf_op jit(solution)/shard_map/jit(_where)/select_n | solution.py:41
  87.3 4.4 %all-to-all-start.1 = ((bf16[8,1365,128]{2,1,0:T(8,128)(2,1)}), bf16[8,1365,128]{2,1,0:T(8,128)(2,1)}, u32[]{:S(2)}, u32[]{:S(2)}) async-start(bf16[8,1365,128]{2,1,0:T(8,128)(2,1)} %select_select_fusion), calls=%async_computation.1 | async-start | bytes 5603328 | tf_op jit(solution)/shard_map/all_to_all | solution.py:42
  91.7 0.0 all-gather.3.cloned.1.call-start
  91.8 34.1 %all-to-all-done.1 = bf16[8,1365,128]{2,1,0:T(8,128)(2,1)} async-done(((bf16[8,1365,128]{2,1,0:T(8,128)(2,1)}), bf16[8,1365,128]{2,1,0:T(8,128)(2,1)}, u32[]{:S(2)}, u32[]{:S(2)}) %all-to-all-start.1) | async-done | bytes 2795552 | tf_op jit(solution)/shard_map/all_to_all | solution.py:42
  125.9 4.2 %reshape.256 = bf16[10920,128]{1,0:T(8,128)(2,1)} reshape(bf16[8,1365,128]{2,1,0:T(8,128)(2,1)} %all-to-all-done.1) | data formatting | bytes 5591040 | tf_op jit(solution)/shard_map/reshape | solution.py:43
  130.1 13.2 %gather_fusion.1 = bf16[4096,128]{1,0:T(8,128)(2,1)S(1)} fusion(bf16[10920,128]{1,0:T(8,128)(2,1)} %reshape.256, s32[4096]{0:T(1024)S(1)} %broadcast_clamp_fusion), kind=kCustom, calls=%fused_computation.1 | custom fusion | bytes 2113536 | tf_op jit(solution)/shard_map/gather | solution.py:43
  143.3 8.7 %copy.57 = bf16[2,2048,128]{2,0,1:T(2,128)(2,1)S(1)} copy(bf16[2,2048,128]{2,1,0:T(8,128)(2,1)S(1)} %bitcast.75) | data formatting | bytes 2097152 | tf_op jit(solution)/shard_map/reshape | solution.py:44
  152.0 27.2 %all_to_all.24 = bf16[2,2048,128]{2,0,1:T(2,128)(2,1)S(1)} all-to-all(bf16[2,2048,128]{2,0,1:T(2,128)(2,1)S(1)} %copy.57), channel_id=1, replica_groups=mesh['rows'=8,'cols'=4] {'cols'}, dimensions={1} | all-to-all | bytes 2097152 | tf_op jit(solution)/shard_map/all_to_all | solution.py:45
  179.2 0.0 copy-start.2
  179.2 1.5 copy_convert_fusion
  180.7 2.9 copy.59
  183.6 0.6 multiply_reduce_fusion
  184.3 0.0 copy-done.2
  184.3 1.8 fusion.18
  186.2 3.2 convolution_convert_fusion
  189.4 0.0 copy-start.3
  189.4 1.7 fusion.44
  191.1 0.0 all-gather.3.cloned.1.call-update
  191.1 0.0 all-gather.5.cloned.1.call-start
  191.2 0.0 copy-done.3
  191.2 0.1 iota_compare_fusion.3
  191.3 0.7 iota_compare_fusion
  191.9 2.6 broadcast_and_fusion
  194.6 1.3 copy.61
  195.9 0.0 all-gather.5.cloned.1.call-update
  195.9 76.4 %all-gather.3.cloned.1.call-done = bf16[2,2048,512]{2,1,0:T(8,128)(2,1)} async-done(((bf16[2,512,512]{2,1,0:T(8,128)(2,1)}), bf16[2,2048,512]{2,1,0:T(8,128)(2,1)}) %all-gather.3.cloned.1.call-update) | async-done | bytes 4194320 | tf_op jit(solution)/shard_map/all_gather | solution.py:57
  272.4 6.3 %copy.62 = bf16[2,2048,512]{1,2,0:T(8,128)(2,1)} copy(bf16[2,2048,512]{2,1,0:T(8,128)(2,1)} %all-gather.3.cloned.1.call-done) | data formatting | bytes 8388608 | tf_op jit(solution)/shard_map/all_gather | solution.py:57
  278.6 0.0 copy-start.1
  278.6 27.7 %fusion = (f32[2,8,512]{2,1,0:T(8,128)S(1)}, f32[2,8,512,2048]{3,2,1,0:T(8,128)}) fusion(pred[2,512,2048]{2,1,0:T(8,128)(4,1)} %broadcast_and_fusion, bf16[2,512,8,64]{1,3,2,0:T(8,128)(2,1)} %bitcast.74, bf16[2,2048,8,64]{1,3,2,0:T(8,128)(2,1)} %bitcast.72), kind=kOutput, calls=%fused_computation.5 | convolution fusion | flops 2197807104 | bytes 74481664 | tf_op jit(solution)/shard_map/bqhd,bkhd->bhqk/dot_general | solution.py:63
  306.3 0.0 copy-done.1
  306.3 22.4 %fusion.1 = f32[2,8,512]{2,1,0:T(8,128)S(1)} fusion(f32[2,8,512,2048]{3,2,1,0:T(8,128)} %get-tuple-element.13, f32[2,8,512]{2,1,0:T(8,128)S(1)} %broadcast_maximum_fusion, pred[2,512,2048]{2,1,0:T(8,128)(4,1)S(1)} %copy-done.1), kind=kLoop, calls=%fused_computation.6 | loop fusion | flops 83877888 | bytes 69271552 | tf_op jit(solution)/shard_map/reduce_sum | solution.py:73
  328.7 24.5 %all-gather.5.cloned.1.call-done = bf16[2,2048,512]{2,1,0:T(8,128)(2,1)} async-done(((bf16[2,512,512]{2,1,0:T(8,128)(2,1)}), bf16[2,2048,512]{2,1,0:T(8,128)(2,1)}) %all-gather.5.cloned.1.call-update) | async-done | bytes 4194320 | tf_op jit(solution)/shard_map/all_gather | solution.py:58
  353.2 6.3 %copy.63 = bf16[2,2048,512]{1,2,0:T(8,128)(2,1)} copy(bf16[2,2048,512]{2,1,0:T(8,128)(2,1)} %all-gather.5.cloned.1.call-done) | data formatting | bytes 8388608 | tf_op jit(solution)/shard_map/all_gather | solution.py:58
  359.5 27.0 %fusion.16 = bf16[2,512,8,64]{1,3,2,0:T(8,128)(2,1)S(1)} fusion(bf16[2,2048,8,64]{1,3,2,0:T(8,128)(2,1)} %bitcast.76, f32[2,8,512,2048]{3,2,1,0:T(8,128)} %get-tuple-element.13, f32[2,8,512]{2,1,0:T(8,128)S(1)} %broadcast_maximum_fusion, pred[2,512,2048]{2,1,0:T(8,128)(4,1)} %broadcast_and_fusion, f32[2,512,8]{1,2,0:T(8,128)S(1)} %bitcast.85), kind=kOutput, calls=%fused_computation.28 | convolution fusion | flops 2232418304 | bytes 74514432 | tf_op jit(solution)/shard_map/bhqk,bkhd->bhqd/dot_general | solution.py:74
  386.5 0.0 copy-start.4
  386.5 0.0 copy-start.5
  386.5 2.7 fusion.11
  389.2 0.3 copy-done.4
  389.4 0.0 copy-done.5
  389.4 8.3 %fusion.7 = f32[2,512,4096]{2,1,0:T(8,128)} fusion(bf16[512,4096]{1,0:T(8,128)(2,1)S(1)} %copy-done.4, bf16[2,512,512]{1,2,0:T(8,128)(2,1)S(1)} %get-tuple-element.15, f32[512]{0:T(512)S(1)} %copy-done.5, f32[2,512]{1,0:T(2,128)S(1)} %add_rsqrt_fusion), kind=kOutput, calls=%fused_computation.12 | convolution fusion | flops 4297064448 | bytes 22026240 | tf_op jit(solution)/shard_map/bqe,ef->bqf/dot_general | solution.py:90
  397.8 0.0 copy-done
  397.8 8.6 %fusion.14 = bf16[2,512,512]{1,2,0:T(8,128)(2,1)S(1)} fusion(bf16[2,512,512]{1,2,0:T(8,128)(2,1)S(1)} %get-tuple-element.15, bf16[2048,512]{1,0:T(8,128)(2,1)S(1)} %copy-done, f32[2,512,4096]{2,1,0:T(8,128)} %fusion.7), kind=kOutput, calls=%fused_computation.25 | convolution fusion | flops 2161639424 | bytes 20971520 | tf_op jit(solution)/shard_map/bqf,fe->bqe/dot_general | solution.py:93
  406.3 1.3 copy.68
  (16 shorter events, 0.2 us)
Async XLA Ops:
  6.5 391.2 %copy-start = (bf16[2048,512]{1,0:T(8,128)(2,1)S(1)}, bf16[2048,512]{1,0:T(8,128)(2,1)}, u32[]{:S(2)}) copy-start(bf16[2048,512]{1,0:T(8,128)(2,1)} %param.17) | copy-start | bytes 6291460
  87.3 38.6 %all-to-all-start.1 = ((bf16[8,1365,128]{2,1,0:T(8,128)(2,1)}), bf16[8,1365,128]{2,1,0:T(8,128)(2,1)}, u32[]{:S(2)}, u32[]{:S(2)}) async-start(bf16[8,1365,128]{2,1,0:T(8,128)(2,1)} %select_select_fusion), calls=%async_computation.1 | async-start | bytes 5603328 | tf_op jit(solution)/shard_map/all_to_all | solution.py:42
  91.7 180.7 %all-gather.3.cloned.1.call-start = ((), (), s32[]{:S(2)}) async-start(), calls=%async_computation.3 | async-start | bytes 5242880 | tf_op jit(solution)/shard_map/all_gather | solution.py:57
  179.2 5.1 %copy-start.2 = (f32[512]{0:T(512)S(1)}, f32[512]{0:T(512)}, u32[]{:S(2)}) copy-start(f32[512]{0:T(512)} %param.12) | copy-start | bytes 6148
  189.4 1.8 copy-start.3
  191.1 162.1 %all-gather.5.cloned.1.call-start = ((), (), s32[]{:S(2)}) async-start(), calls=%async_computation.4 | async-start | bytes 5242880 | tf_op jit(solution)/shard_map/all_gather | solution.py:58
  278.6 27.7 %copy-start.1 = (pred[2,512,2048]{2,1,0:T(8,128)(4,1)S(1)}, pred[2,512,2048]{2,1,0:T(8,128)(4,1)}, u32[]{:S(2)}) copy-start(pred[2,512,2048]{2,1,0:T(8,128)(4,1)} %broadcast_and_fusion) | copy-start | bytes 6291460
  386.5 3.0 copy-start.4
  386.5 3.0 copy-start.5
Sparse Core Ops, SparseCore 0:
  191.2 81.0 all-gather.2
  273.9 79.2 all-gather.4
where the time goes:
time: 415 us
  waiting for transfers between devices  135 us (33%)
  local copies, waits for them, and re-layouts  90.2 us (22%)
  matrix products  77.4 us (19%)
  blocking collectives  50.8 us (12%)
  other arithmetic  42.8 us (10%)
  between operations  13.7 us (3%)
  starting transfers between devices  4.49 us (1%)
    all_gather x1, waiting for transfers between devices, local(): key_piece = lax.all_gather(keys, 'cols', axis=1, tiled=True)  76.4 us
    all_to_all x1, waiting for transfers between devices, local(): lax.all_to_all(looked, 'rows', split_axis=0, concat_axis=0, tiled=True)  34.1 us
    gather x2, local copies, waits for them, and re-layouts, local(): looked = jnp.take(table, jnp.maximum(asked, 0), axis=0)  27.9 us
    dot_general x1, matrix products, local(): jnp.einsum('bqhd,bkhd->bhqk', queries, key_heads, preferred_element_type=...  27.7 us
    all_to_all x1, blocking collectives, local(): lax.all_to_all(embedded, 'cols', split_axis=1, concat_axis=2, tiled=True)  27.2 us
    dot_general x1, matrix products, local(): jnp.einsum('bhqk,bkhd->bhqd', probs.astype(jnp.bfloat16), value_heads, pr...  27 us
    all_gather x1, waiting for transfers between devices, local(): value_piece = lax.all_gather(values, 'cols', axis=1, tiled=True)  24.5 us
    reduce_sum x1, other arithmetic, local(): running_sum = jnp.sum(probs, axis=-1)  22.4 us
  transfers between devices with their start and end apart: 3, of which 3 were waited for; matrix products, arithmetic and copies ran while one was open for 15% of the time, Pallas kernels for 0%

commit v1 on v0

--- a/solution.py
+++ b/solution.py
@@ -6,6 +6,19 @@
 D = 512
 HEADS = 8
 FF = 2048
+
+
+def gather_around(value, axis, dim):
+    ways = lax.axis_size(axis)
+    up = [(d, (d + 1) % ways) for d in range(ways)]
+    down = [(d, (d - 1) % ways) for d in range(ways)]
+    earlier, later = ([value], [value])
+    for _ in range(ways // 2):
+        earlier.append(lax.ppermute(earlier[-1], axis, up))
+    for _ in range((ways - 1) // 2):
+        later.append(lax.ppermute(later[-1], axis, down))
+    line = jnp.concatenate([*earlier[::-1], *later[1:]], axis=dim)
+    return jnp.roll(line, (lax.axis_index(axis) - ways // 2) * value.shape[dim], axis=dim)
 
 
 def rms_norm(values_f32, gain):
@@ -55,7 +68,7 @@
     query_pos = lax.axis_index("cols") * quarter + jnp.arange(quarter, dtype=jnp.int32)
     running_max = jnp.full((batch_dev, HEADS, quarter), -1e30, jnp.float32)
     key_piece = lax.all_gather(keys, "cols", axis=1, tiled=True)
-    value_piece = lax.all_gather(values, "cols", axis=1, tiled=True)
+    value_piece = gather_around(values, "cols", 1)
     piece_len = key_piece.shape[1]
     key_heads = key_piece.reshape(batch_dev, piece_len, HEADS, head_dim)
     value_heads = value_piece.reshape(batch_dev, piece_len, HEADS, head_dim)

time: 415 us -> 460 us (1.11)
  waiting for transfers between devices: 135 us -> 166 us
  local copies, waits for them, and re-layouts: 90.2 us -> 100 us
    ppermute x0 -> x3, waiting for transfers between devices: none -> 65.4 us  [the longest x2 48.6 us: gather_around(): earlier.append(lax.ppermute(earlier[-1], axis, up))]
    all_gather x1 -> x0, waiting for transfers between devices: 24.5 us -> none  [local(): value_piece = lax.all_gather(values, 'cols', axis=1, tiled=True)]
    dynamic_slice x0 -> x2, local copies, waits for them, and re-layouts: none -> 10.9 us  [gather_around(): jnp.roll(line, (lax.axis_index(axis) - ways // 2) * value.shape[dim], axi...]
    all_gather x1, waiting for transfers between devices: 76.4 us -> 66.6 us  [local(): key_piece = lax.all_gather(keys, 'cols', axis=1, tiled=True)]
    all_gather x1 -> x0, local copies, waits for them, and re-layouts: 6.28 us -> none  [local(): value_piece = lax.all_gather(values, 'cols', axis=1, tiled=True)]
  transfers between devices with their start and end apart: 3 -> 5, of which waited for: 3 -> 5; matrix products, arithmetic and copies ran while one was open for 15% -> 4% of each run, Pallas kernels for 0% -> 0%
where the time goes in v1:
time: 460 us; the launch traced here: 459 us
  waiting for transfers between devices  166 us (36%)
  local copies, waits for them, and re-layouts  100 us (22%)
  matrix products  76.8 us (17%)
  blocking collectives  50.8 us (11%)
  other arithmetic  42.8 us (9%)
  between operations  13.7 us (3%)
  starting transfers between devices  8.54 us (2%)
    all_gather x1, waiting for transfers between devices, local(): key_piece = lax.all_gather(keys, 'cols', axis=1, tiled=True)  66.6 us
    ppermute x2, waiting for transfers between devices, gather_around(): earlier.append(lax.ppermute(earlier[-1], axis, up))  48.6 us
    all_to_all x1, waiting for transfers between devices, local(): lax.all_to_all(looked, 'rows', split_axis=0, concat_axis=0, tiled=True)  34.1 us
    gather x2, local copies, waits for them, and re-layouts, local(): looked = jnp.take(table, jnp.maximum(asked, 0), axis=0)  27.9 us
    all_to_all x1, blocking collectives, local(): lax.all_to_all(embedded, 'cols', split_axis=1, concat_axis=2, tiled=True)  27.2 us
    dot_general x1, matrix products, local(): jnp.einsum('bqhd,bkhd->bhqk', queries, key_heads, preferred_element_type=...  27.1 us
    dot_general x1, matrix products, local(): jnp.einsum('bhqk,bkhd->bhqd', probs.astype(jnp.bfloat16), value_heads, pr...  26.9 us
    reduce_sum x1, other arithmetic, local(): running_sum = jnp.sum(probs, axis=-1)  22.4 us
  transfers between devices with their start and end apart: 5, of which 5 were waited for; matrix products, arithmetic and copies ran while one was open for 4% of the time, Pallas kernels for 0%

profile of v1, /device:TPU:0, one launch (start us, length us, event | category | flops | bytes accessed | tf_op | source)
XLA Modules:
  0.0 459.3 jit_solution(13227516693580612674)
XLA Ops:
  6.5 0.0 copy-start
  6.5 15.2 %all_gather.6 = s32[2,2048]{1,0:T(2,128)S(1)} all-gather(s32[2,512]{1,0:T(2,128)} %param.9), channel_id=1, replica_groups=mesh['rows'=8,'cols'=4] {'cols'}, dimensions={1}, use_global_device_ids=true | all-gather | bytes 20480 | tf_op jit(solution)/shard_map/all_gather | solution.py:36
  21.8 2.3 reduce-window.6
  24.1 0.3 slice_reduce_fusion
  24.5 0.2 reduce-window.9
  24.6 0.1 add_bitcast_fusion
  24.8 0.1 fusion.32
  24.9 0.1 compare_select_fusion
  25.0 15.5 %scatter_custom_fusion = s32[10920]{0:T(1024)S(1)} fusion(s32[4096]{0:T(1024)S(1)} %bitcast.82, s32[4096]{0:T(1024)S(1)} %get-tuple-element.10, s32[]{:T(128)} %constant.74.clone.1), kind=kCustom, calls=%fused_computation.65 | custom fusion | bytes 43684 | tf_op jit(solution)/shard_map/scatter | solution.py:49
  40.5 0.1 all_to_all.16
  40.6 8.4 %all_to_all.23 = s32[8,1,1365]{2,1,0:T(1,128)S(1)} all-to-all(s32[8,1,1365]{2,1,0:T(1,128)S(1)} %all_to_all.16), channel_id=1, replica_groups=mesh['rows'=8,'cols'=4] {'rows'}, dimensions={0} | all-to-all | bytes 87360 | tf_op jit(solution)/shard_map/all_to_all | solution.py:52
  49.1 0.1 reshape.265
  49.2 23.7 %gather_fusion = bf16[10920,128]{1,0:T(8,128)(2,1)} fusion(bf16[16384,128]{1,0:T(8,128)(2,1)} %param.11, s32[11264]{0:T(1024)S(1)} %pad_clamp_fusion), kind=kCustom, calls=%fused_computation | custom fusion | bytes 5634720 | tf_op jit(solution)/shard_map/jit(_take)/gather | solution.py:53
  72.9 4.2 reshape.264
  77.1 10.2 %select_select_fusion = bf16[8,1365,128]{2,1,0:T(8,128)(2,1)} fusion(bf16[8,1365,128]{2,1,0:T(8,128)(2,1)} %reshape.264, pred[8,1365]{1,0:T(8,128)(4,1)S(1)} %get-tuple-element.9, pred[8,1365]{1,0:T(8,128)(4,1)S(1)} %get-tuple-element.8), kind=kLoop, calls=%fused_computation.21 | loop fusion | flops 2795520 | bytes 5612880 | tf_op jit(solution)/shard_map/jit(_where)/select_n | solution.py:54
  87.3 4.4 all-to-all-start.1
  91.7 0.0 all-gather.2.cloned.1.call-start
  91.8 34.1 %all-to-all-done.1 = bf16[8,1365,128]{2,1,0:T(8,128)(2,1)} async-done(((bf16[8,1365,128]{2,1,0:T(8,128)(2,1)}), bf16[8,1365,128]{2,1,0:T(8,128)(2,1)}, u32[]{:S(2)}, u32[]{:S(2)}) %all-to-all-start.1) | async-done | bytes 2795552 | tf_op jit(solution)/shard_map/all_to_all | solution.py:55
  125.9 4.2 reshape.256
  130.1 13.2 %gather_fusion.1 = bf16[4096,128]{1,0:T(8,128)(2,1)S(1)} fusion(bf16[10920,128]{1,0:T(8,128)(2,1)} %reshape.256, s32[4096]{0:T(1024)S(1)} %broadcast_clamp_fusion), kind=kCustom, calls=%fused_computation.1 | custom fusion | bytes 2113536 | tf_op jit(solution)/shard_map/gather | solution.py:56
  143.3 8.7 %copy.56 = bf16[2,2048,128]{2,0,1:T(2,128)(2,1)S(1)} copy(bf16[2,2048,128]{2,1,0:T(8,128)(2,1)S(1)} %bitcast.76) | data formatting | bytes 2097152 | tf_op jit(solution)/shard_map/reshape | solution.py:57
  152.0 27.2 %all_to_all.24 = bf16[2,2048,128]{2,0,1:T(2,128)(2,1)S(1)} all-to-all(bf16[2,2048,128]{2,0,1:T(2,128)(2,1)S(1)} %copy.56), channel_id=1, replica_groups=mesh['rows'=8,'cols'=4] {'cols'}, dimensions={1} | all-to-all | bytes 2097152 | tf_op jit(solution)/shard_map/all_to_all | solution.py:58
  179.2 0.6 multiply_reduce_fusion
  179.9 1.5 copy_convert_fusion
  181.4 2.9 copy.58
  184.3 1.8 fusion.18
  186.2 3.2 convolution_convert_fusion
  189.4 0.1 slice.35
  189.5 0.3 collective-permute-start
  189.8 24.6 %collective-permute-done = bf16[2,512,512]{2,1,0:T(8,128)(2,1)S(1)} collective-permute-done((bf16[2,512,512]{2,1,0:T(8,128)(2,1)S(1)}, bf16[2,512,512]{2,1,0:T(8,128)(2,1)S(1)}, u32[]{:S(2)}, u32[]{:S(2)}) %collective-permute-start) | collective-permute-done | bytes 1048608 | tf_op jit(solution)/shard_map/ppermute | solution.py:17
  214.4 0.0 collective-permute-start.1
  214.4 3.8 collective-permute-start.2
  218.2 24.0 %collective-permute-done.1 = bf16[2,512,512]{2,1,0:T(8,128)(2,1)S(1)} collective-permute-done((bf16[2,512,512]{2,1,0:T(8,128)(2,1)S(1)}, bf16[2,512,512]{2,1,0:T(8,128)(2,1)S(1)}, u32[]{:S(2)}, u32[]{:S(2)}) %collective-permute-start.1) | collective-permute-done | bytes 1048608 | tf_op jit(solution)/shard_map/ppermute | solution.py:17
  242.2 0.1 constant_dynamic-update-slice_fusion.7
  242.3 0.1 constant_dynamic-update-slice_fusion.6
  242.3 0.1 constant_dynamic-update-slice_fusion.5
  242.4 16.8 %collective-permute-done.2 = bf16[2,512,512]{2,1,0:T(8,128)(2,1)S(1)} collective-permute-done((bf16[2,512,512]{2,1,0:T(8,128)(2,1)S(1)}, bf16[2,512,512]{2,1,0:T(8,128)(2,1)S(1)}, u32[]{:S(2)}, u32[]{:S(2)}) %collective-permute-start.2) | collective-permute-done | bytes 1048608 | tf_op jit(solution)/shard_map/ppermute | solution.py:19
  259.2 0.1 constant_dynamic-update-slice_fusion.4
  259.3 0.1 constant_dynamic-update-slice_fusion.3
  259.4 0.1 constant_dynamic-update-slice_fusion.2
  259.5 0.0 copy-start.4
  259.5 1.6 fusion.44
  261.1 3.2 copy-done.2
  264.3 0.0 all-gather.2.cloned.1.call-update
  264.4 0.1 iota_compare_fusion.3
  264.5 0.7 iota_compare_fusion
  265.1 2.6 broadcast_and_fusion
  267.8 2.4 copy.60
  270.1 1.0 constant_dynamic-update-slice_fusion
  271.2 4.4 constant_dynamic-slice_fusion
  275.6 6.5 %copy.62 = bf16[2,2048,512]{1,2,0:T(8,128)(2,1)} copy(bf16[2,2048,512]{2,1,0:T(8,128)(2,1)} %constant_dynamic-slice_fusion) | data formatting | bytes 8388608 | tf_op jit(solution)/shard_map/jit(_roll_dynamic)/dynamic_slice | solution.py:21
  282.0 66.6 %all-gather.2.cloned.1.call-done = bf16[2,2048,512]{2,1,0:T(8,128)(2,1)} async-done(((bf16[2,512,512]{2,1,0:T(8,128)(2,1)}), bf16[2,2048,512]{2,1,0:T(8,128)(2,1)}) %all-gather.2.cloned.1.call-update) | async-done | bytes 4194320 | tf_op jit(solution)/shard_map/all_gather | solution.py:70
  348.6 6.3 %copy.61 = bf16[2,2048,512]{1,2,0:T(8,128)(2,1)} copy(bf16[2,2048,512]{2,1,0:T(8,128)(2,1)} %all-gather.2.cloned.1.call-done) | data formatting | bytes 8388608 | tf_op jit(solution)/shard_map/all_gather | solution.py:70
  354.9 27.1 %fusion = (f32[2,8,512]{2,1,0:T(8,128)S(1)}, f32[2,8,512,2048]{3,2,1,0:T(8,128)}) fusion(pred[2,512,2048]{2,1,0:T(8,128)(4,1)} %broadcast_and_fusion, bf16[2,512,8,64]{1,3,2,0:T(8,128)(2,1)} %bitcast.75, bf16[2,2048,8,64]{1,3,2,0:T(8,128)(2,1)} %bitcast.73), kind=kOutput, calls=%fused_computation.5 | convolution fusion | flops 2197807104 | bytes 74481664 | tf_op jit(solution)/shard_map/bqhd,bkhd->bhqk/dot_general | solution.py:76
  382.0 22.4 %fusion.1 = f32[2,8,512]{2,1,0:T(8,128)S(1)} fusion(f32[2,8,512,2048]{3,2,1,0:T(8,128)} %get-tuple-element.13, f32[2,8,512]{2,1,0:T(8,128)S(1)} %broadcast_maximum_fusion, pred[2,512,2048]{2,1,0:T(8,128)(4,1)S(1)} %copy-done.1), kind=kLoop, calls=%fused_computation.6 | loop fusion | flops 83877888 | bytes 69271552 | tf_op jit(solution)/shard_map/reduce_sum | solution.py:86
  404.3 26.9 %fusion.16 = bf16[2,512,8,64]{1,3,2,0:T(8,128)(2,1)S(1)} fusion(bf16[2,2048,8,64]{1,3,2,0:T(8,128)(2,1)} %bitcast.77, f32[2,8,512,2048]{3,2,1,0:T(8,128)} %get-tuple-element.13, f32[2,8,512]{2,1,0:T(8,128)S(1)} %broadcast_maximum_fusion, pred[2,512,2048]{2,1,0:T(8,128)(4,1)} %broadcast_and_fusion, f32[2,512,8]{1,2,0:T(8,128)S(1)} %bitcast.86), kind=kOutput, calls=%fused_computation.28 | convolution fusion | flops 2232418304 | bytes 74514432 | tf_op jit(solution)/shard_map/bhqk,bkhd->bhqd/dot_general | solution.py:87
  431.2 0.0 copy-start.5
  431.3 0.0 copy-start.6
  431.3 2.7 fusion.11
  434.0 0.3 copy-done.5
  434.2 0.0 copy-done.6
  434.2 8.3 %fusion.7 = f32[2,512,4096]{2,1,0:T(8,128)} fusion(bf16[512,4096]{1,0:T(8,128)(2,1)S(1)} %copy-done.5, bf16[2,512,512]{1,2,0:T(8,128)(2,1)S(1)} %get-tuple-element.15, f32[512]{0:T(512)S(1)} %copy-done.6, f32[2,512]{1,0:T(2,128)S(1)} %add_rsqrt_fusion), kind=kOutput, calls=%fused_computation.12 | convolution fusion | flops 4297064448 | bytes 22026240 | tf_op jit(solution)/shard_map/bqe,ef->bqf/dot_general | solution.py:103
  442.6 8.6 %fusion.14 = bf16[2,512,512]{1,2,0:T(8,128)(2,1)S(1)} fusion(bf16[2,512,512]{1,2,0:T(8,128)(2,1)S(1)} %get-tuple-element.15, bf16[2048,512]{1,0:T(8,128)(2,1)S(1)} %copy-done, f32[2,512,4096]{2,1,0:T(8,128)} %fusion.7), kind=kOutput, calls=%fused_computation.25 | convolution fusion | flops 2161639424 | bytes 20971520 | tf_op jit(solution)/shard_map/bqf,fe->bqe/dot_general | solution.py:106
  451.1 1.3 copy.67
  (23 shorter events, 0.2 us)
Async XLA Ops:
  6.5 436.0 %copy-start = (bf16[2048,512]{1,0:T(8,128)(2,1)S(1)}, bf16[2048,512]{1,0:T(8,128)(2,1)}, u32[]{:S(2)}) copy-start(bf16[2048,512]{1,0:T(8,128)(2,1)} %param.17) | copy-start | bytes 6291460
  87.3 38.6 %all-to-all-start.1 = ((bf16[8,1365,128]{2,1,0:T(8,128)(2,1)}), bf16[8,1365,128]{2,1,0:T(8,128)(2,1)}, u32[]{:S(2)}, u32[]{:S(2)}) async-start(bf16[8,1365,128]{2,1,0:T(8,128)(2,1)} %select_select_fusion), calls=%async_computation.1 | async-start | bytes 5603328 | tf_op jit(solution)/shard_map/all_to_all | solution.py:55
  91.7 256.9 %all-gather.2.cloned.1.call-start = ((), (), s32[]{:S(2)}) async-start(), calls=%async_computation.3 | async-start | bytes 5242880 | tf_op jit(solution)/shard_map/all_gather | solution.py:70
  179.2 5.1 %copy-start.3 = (f32[512]{0:T(512)S(1)}, f32[512]{0:T(512)}, u32[]{:S(2)}) copy-start(f32[512]{0:T(512)} %param.12) | copy-start | bytes 6148
  189.5 24.9 %collective-permute-start = (bf16[2,512,512]{2,1,0:T(8,128)(2,1)S(1)}, bf16[2,512,512]{2,1,0:T(8,128)(2,1)S(1)}, u32[]{:S(2)}, u32[]{:S(2)}) collective-permute-start(bf16[2,512,512]{2,1,0:T(8,128)(2,1)S(1)} %slice.35), channel_id=1, source_target_pairs={{0,1},{1,2},{2,3},{3,0},{4,5},{5,6},{6,7},{7,4},{8,9},{9,10},{10,1... | collective-permute-start | bytes 3145736 | tf_op jit(solution)/shard_map/ppermute | solution.py:17
  214.4 27.8 %collective-permute-start.1 = (bf16[2,512,512]{2,1,0:T(8,128)(2,1)S(1)}, bf16[2,512,512]{2,1,0:T(8,128)(2,1)S(1)}, u32[]{:S(2)}, u32[]{:S(2)}) collective-permute-start(bf16[2,512,512]{2,1,0:T(8,128)(2,1)S(1)} %collective-permute-done), channel_id=1, source_target_pairs={{0,1},{1,2},{2,3},{3,0},{4,5},{5,6},{6,7},{7,4},{8,9},{9,10},{10,1... | collective-permute-start | bytes 3145736 | tf_op jit(solution)/shard_map/ppermute | solution.py:17
  214.4 44.9 %collective-permute-start.2 = (bf16[2,512,512]{2,1,0:T(8,128)(2,1)S(1)}, bf16[2,512,512]{2,1,0:T(8,128)(2,1)S(1)}, u32[]{:S(2)}, u32[]{:S(2)}) collective-permute-start(bf16[2,512,512]{2,1,0:T(8,128)(2,1)S(1)} %slice.35), channel_id=1, source_target_pairs={{0,3},{1,0},{2,1},{3,2},{4,7},{5,4},{6,5},{7,6},{8,11},{9,8},{10,9... | collective-permute-start | bytes 3145736 | tf_op jit(solution)/shard_map/ppermute | solution.py:19
  259.5 4.9 %copy-start.4 = (s32[2]{0:T(128)S(1)}, s32[2]{0:T(128)}, u32[]{:S(2)}) copy-start(s32[2]{0:T(128)} %param.10) | copy-start | bytes 28
  261.1 3.2 copy-start.2
  354.9 27.1 %copy-start.1 = (pred[2,512,2048]{2,1,0:T(8,128)(4,1)S(1)}, pred[2,512,2048]{2,1,0:T(8,128)(4,1)}, u32[]{:S(2)}) copy-start(pred[2,512,2048]{2,1,0:T(8,128)(4,1)} %broadcast_and_fusion) | copy-start | bytes 6291460
  431.2 3.0 copy-start.5
  431.3 3.0 copy-start.6
Sparse Core Ops, SparseCore 0:
  264.5 84.0 all-gather.1
